TPU v7x, 32 devices: a whole 2x2x4 slice. The times are simulated.
32 devices in a mesh: fsdp: 4 (over z), ctx: 2 (over x), tp: 4 (over y, core).
Axes of the slice: x: 2, y: 2, z: 4, core: 2. Of those that a mesh axis runs over, the one named last changes fastest.
Arguments:
- residual: bfloat16 [8, 1024, 1024], P('fsdp', ('ctx', 'tp')), may hold values from -6 to 6
- query_weight: bfloat16 [1024, 1024], P('fsdp', 'tp'), may hold values from -0.1875 to 0.1875
- key_weight: bfloat16 [1024, 1024], P('fsdp', 'tp'), may hold values from -0.1875 to 0.1875
- value_weight: bfloat16 [1024, 1024], P('fsdp', 'tp'), may hold values from -0.1875 to 0.1875
- output_weight: bfloat16 [1024, 1024], P('tp', 'fsdp'), may hold values from -0.1875 to 0.1875
- sharpness: float32 [1024], P('tp'), may hold values from 1 to 1.8
- attend_rate: float32 [1024], replicated, may hold values from 0.15 to 0.9
- up_weight: bfloat16 [1024, 4096], P('fsdp', 'tp'), may hold values from -0.1875 to 0.1875
- gate_weight: bfloat16 [1024, 4096], P('fsdp', 'tp'), may hold values from -0.1875 to 0.1875
- down_weight: bfloat16 [4096, 1024], P('tp', 'fsdp'), may hold values from -0.09375 to 0.09375
- amplitude: float32 [4096], P('tp'), may hold values from 0.5 to 2
- steepness: float32 [4096], P('tp'), may hold values from 0.5 to 2
- mixer_rate: float32 [1024], replicated, may hold values from 0.15 to 0.9
- block_ids: int32 [8, 1024], P('fsdp'), may hold values from 0 to 4, as said below
- positions: int32 [8, 1024], P('fsdp', 'ctx'), may hold values from 0 to 4095
- cotangent: bfloat16 [8, 1024, 1024], P('fsdp', ('ctx', 'tp')), may hold values from -6 to 6
Outputs:
- layer_out: bfloat16 [8, 1024, 1024], P('fsdp', ('ctx', 'tp'))
- grad_input: float32 [8, 1024, 1024], P('fsdp', ('ctx', 'tp'))
- grad_query: float32 [1024, 1024], P('fsdp', 'tp')
- grad_key: float32 [1024, 1024], P('fsdp', 'tp')
- grad_value: float32 [1024, 1024], P('fsdp', 'tp')
- grad_output: float32 [1024, 1024], P('tp', 'fsdp')
- grad_sharpness: float32 [1024], replicated
- grad_attend: float32 [1024], replicated
- grad_up: float32 [1024, 4096], P('fsdp', 'tp')
- grad_gate: float32 [1024, 4096], P('fsdp', 'tp')
- grad_down: float32 [4096, 1024], P('tp', 'fsdp')
- grad_amplitude: float32 [4096], replicated
- grad_steepness: float32 [4096], replicated
- grad_mixer: float32 [1024], replicated
Inputs may be any that keep to these rules, and one draw needn't show every extreme that they name: `block_ids`: in each sequence the block id of the token at index t is (t + offset) // 256, with an offset of 1 to 255 drawn for each sequence: full blocks of 256 tokens, a shorter first and last block.
All inputs are finite; a program needn't handle non-finite values.
Results may differ from a plain program's by a relative error of at most 0.02.
Values may be sent and summed in bfloat16 or wider, within the bound.
A program may use at most 128 MiB of HBM per device.

v0:
```python
import math

import jax
import jax.numpy as jnp
from jax import lax
from jax.sharding import PartitionSpec as P

D = 1024
HD = 64
FF = 4096


norm_eps = 1e-06
rope_base = 10000.0


def unit_rows(values):
    return values * lax.rsqrt(jnp.mean(values * values, axis=-1, keepdims=True) + norm_eps)


def rotate_pairs(values, angles):
    middle = values.shape[-1] // 2
    leading = values[..., :middle]
    trailing = values[..., middle:]
    cosine = jnp.cos(angles)[..., None, :]
    sine_part = jnp.sin(angles)[..., None, :]
    return jnp.concatenate(
        [leading * cosine - trailing * sine_part, trailing * cosine + leading * sine_part], axis=-1
    )


def angles_for(positions, head_size):
    middle = head_size // 2
    frequency = rope_base ** (-2.0 * jnp.arange(middle).astype(jnp.float32) / head_size)
    return positions.astype(jnp.float32)[..., None] * frequency


def prepare_heads(projected, angles, gains, head_size):
    heads_here = projected.shape[-1] // head_size
    shaped = projected.reshape(projected.shape[:-1] + (heads_here, head_size))
    normed = unit_rows(rotate_pairs(shaped, angles)) * gains.reshape(heads_here, head_size)
    return normed.reshape(projected.shape)


def product(left, right):
    return jnp.dot(left, right, preferred_element_type=jnp.float32)


def transposed_left(left, right):
    return lax.dot_general(
        left, right, (((0,), (0,)), ((), ())), preferred_element_type=jnp.float32
    )


def transposed_right(left, right):
    return lax.dot_general(
        left, right, (((1,), (1,)), ((), ())), preferred_element_type=jnp.float32
    )


def gather_rows(values):
    return lax.all_gather(values, "tp", axis=1, tiled=True)


def reduce_rows(values):
    return lax.psum_scatter(values, "tp", scatter_dimension=1, tiled=True)


def branch_mix(branch, base, rate):
    return unit_rows(base + rate * (unit_rows(branch) - base))


def activate(upper, gated_raw, amplitude, steepness):
    scaled = gated_raw * steepness
    return upper * amplitude * (scaled * jax.nn.sigmoid(scaled))


def per_device(
    residual,
    query_weight,
    key_weight,
    value_weight,
    output_weight,
    sharpness,
    attend_rate,
    up_weight,
    gate_weight,
    down_weight,
    amplitude,
    steepness,
    mixer_rate,
    block_ids,
    positions,
    cotangent,
):
    full_query, full_key, full_value, full_output, full_up, full_gate, full_down = (
        lax.all_gather(query_weight, "fsdp", axis=0, tiled=True),
        lax.all_gather(key_weight, "fsdp", axis=0, tiled=True),
        lax.all_gather(value_weight, "fsdp", axis=0, tiled=True),
        lax.all_gather(output_weight, "fsdp", axis=1, tiled=True),
        lax.all_gather(up_weight, "fsdp", axis=0, tiled=True),
        lax.all_gather(gate_weight, "fsdp", axis=0, tiled=True),
        lax.all_gather(down_weight, "fsdp", axis=1, tiled=True),
    )
    seqs_here = residual.shape[0]
    model_width = residual.shape[2]
    local_rows = positions.shape[1]
    head_size = HD
    root_size = math.sqrt(head_size)
    context = lax.axis_index("ctx")
    own_ids = lax.dynamic_slice_in_dim(block_ids, context * local_rows, local_rows, 1)
    angles = angles_for(positions, head_size)
    gathered = gather_rows(residual)
    flat_in = gathered.reshape(-1, model_width)
    raw_query = product(flat_in, full_query).reshape(seqs_here, local_rows, -1)
    raw_key = product(flat_in, full_key).reshape(seqs_here, local_rows, -1)
    raw_value = product(flat_in, full_value).reshape(seqs_here, local_rows, -1)

    def prepare_local(projected, gains):
        return prepare_heads(projected, angles, gains, head_size)

    query_ready, query_back = jax.vjp(prepare_local, raw_query, sharpness)
    key_ready, key_back = jax.vjp(prepare_local, raw_key, sharpness)
    query_low = query_ready.astype(jnp.bfloat16)
    key_low = key_ready.astype(jnp.bfloat16)
    value_low = raw_value.astype(jnp.bfloat16)
    key_all, value_all = (
        lax.all_gather(key_low, "ctx", axis=1, tiled=True),
        lax.all_gather(value_low, "ctx", axis=1, tiled=True),
    )

    def visible_scores(seq_query, seq_key, query_ids, key_ids):
        heads_here = seq_query.shape[-1] // head_size
        shaped_query = seq_query.reshape(seq_query.shape[0], heads_here, head_size)
        shaped_key = seq_key.reshape(seq_key.shape[0], heads_here, head_size)
        scores = (
            jnp.einsum("qhd,khd->hqk", shaped_query, shaped_key, preferred_element_type=jnp.float32)
            / root_size
        )
        allowed = key_ids[None, :] <= query_ids[:, None]
        return (jnp.where(allowed[None], scores, -1e30), shaped_query, shaped_key)

    def attend_forward(operands):
        seq_query, seq_key, seq_value, query_ids, key_ids = operands
        scores, shaped_query, shaped_key = visible_scores(seq_query, seq_key, query_ids, key_ids)
        shaped_value = seq_value.reshape(shaped_key.shape)
        row_max = jnp.max(scores, axis=-1, keepdims=True)
        exponent = jnp.exp(scores - row_max)
        row_total = jnp.sum(exponent, axis=-1, keepdims=True)
        weights_low = (exponent / row_total).astype(jnp.bfloat16)
        attended_seq = jnp.einsum(
            "hqk,khd->qhd", weights_low, shaped_value, preferred_element_type=jnp.float32
        )
        return (
            attended_seq.reshape(seq_query.shape).astype(jnp.bfloat16),
            (row_max + jnp.log(row_total))[..., 0],
        )

    attended, logsum = lax.map(attend_forward, (query_low, key_all, value_all, own_ids, block_ids))
    attend_flat = attended.reshape(-1, attended.shape[-1])
    attend_sum = reduce_rows(
        product(attend_flat, full_output).reshape(seqs_here, local_rows, model_width)
    )
    residual_float = residual.astype(jnp.float32)
    first, attend_back = jax.vjp(branch_mix, attend_sum, residual_float, attend_rate)
    first_all = gather_rows(first.astype(jnp.bfloat16))
    flat_first = first_all.reshape(-1, model_width)
    up_raw = product(flat_first, full_up)
    gate_raw = product(flat_first, full_gate)
    hidden, activate_back = jax.vjp(activate, up_raw, gate_raw, amplitude, steepness)
    hidden_low = hidden.astype(jnp.bfloat16)
    down_sum = reduce_rows(
        product(hidden_low, full_down).reshape(seqs_here, local_rows, model_width)
    )
    outcome, mixer_back = jax.vjp(branch_mix, down_sum, first, mixer_rate)
    layer_out = outcome.astype(jnp.bfloat16)
    grad_down_sum, grad_first, grad_mixer_part = mixer_back(cotangent.astype(jnp.float32))
    down_grad_all = gather_rows(grad_down_sum.astype(jnp.bfloat16)).reshape(-1, model_width)
    grad_hidden = transposed_right(down_grad_all, full_down)
    grad_down_part = transposed_left(hidden_low, down_grad_all)
    grad_up_raw, grad_gate_raw, grad_amplitude_part, grad_steepness_part = activate_back(
        grad_hidden
    )
    up_grad_low = grad_up_raw.astype(jnp.bfloat16)
    gate_grad_low = grad_gate_raw.astype(jnp.bfloat16)
    first_back = transposed_right(up_grad_low, full_up) + transposed_right(gate_grad_low, full_gate)
    grad_first = grad_first + reduce_rows(first_back.reshape(seqs_here, local_rows, model_width))
    grad_up_part = transposed_left(flat_first, up_grad_low)
    grad_gate_part = transposed_left(flat_first, gate_grad_low)
    grad_attend_sum, grad_residual, grad_attend_part = attend_back(grad_first)
    attend_grad_all = gather_rows(grad_attend_sum.astype(jnp.bfloat16)).reshape(-1, model_width)
    grad_output_part = transposed_left(attend_flat, attend_grad_all)
    grad_attended = transposed_right(attend_grad_all, full_output).astype(jnp.bfloat16)
    grad_attended = grad_attended.reshape(seqs_here, local_rows, -1)

    def attend_backward(operands):
        seq_query, seq_key, seq_value, query_ids, key_ids, seq_logsum, seq_grad = operands
        scores, shaped_query, shaped_key = visible_scores(seq_query, seq_key, query_ids, key_ids)
        shaped_value = seq_value.reshape(shaped_key.shape)
        shaped_grad = seq_grad.reshape(shaped_query.shape)
        softmax_out = jnp.exp(scores - seq_logsum[..., None])
        grad_value_seq = jnp.einsum(
            "hqk,qhd->khd",
            softmax_out.astype(jnp.bfloat16),
            shaped_grad,
            preferred_element_type=jnp.float32,
        )
        grad_weights = jnp.einsum(
            "qhd,khd->hqk", shaped_grad, shaped_value, preferred_element_type=jnp.float32
        )
        grad_scores = softmax_out * (
            grad_weights - jnp.sum(grad_weights * softmax_out, axis=-1, keepdims=True)
        )
        scores_low = grad_scores.astype(jnp.bfloat16)
        grad_query_seq = (
            jnp.einsum("hqk,khd->qhd", scores_low, shaped_key, preferred_element_type=jnp.float32)
            / root_size
        )
        grad_key_seq = (
            jnp.einsum("hqk,qhd->khd", scores_low, shaped_query, preferred_element_type=jnp.float32)
            / root_size
        )
        return (
            grad_query_seq.reshape(seq_query.shape),
            grad_key_seq.reshape(seq_key.shape),
            grad_value_seq.reshape(seq_key.shape),
        )

    grad_query_ready, grad_key_whole, grad_value_whole = lax.map(
        attend_backward, (query_low, key_all, value_all, own_ids, block_ids, logsum, grad_attended)
    )
    grad_key_ready, grad_value_ready = (
        lax.psum_scatter(
            grad_key_whole.astype(jnp.bfloat16), "ctx", scatter_dimension=1, tiled=True
        ).astype(jnp.float32),
        lax.psum_scatter(
            grad_value_whole.astype(jnp.bfloat16), "ctx", scatter_dimension=1, tiled=True
        ).astype(jnp.float32),
    )
    grad_raw_query, sharp_query = query_back(grad_query_ready)
    grad_raw_key, sharp_key = key_back(grad_key_ready)
    query_grad_low = grad_raw_query.astype(jnp.bfloat16).reshape(-1, grad_raw_query.shape[-1])
    key_grad_low = grad_raw_key.astype(jnp.bfloat16).reshape(-1, grad_raw_key.shape[-1])
    value_grad_low = grad_value_ready.astype(jnp.bfloat16).reshape(-1, grad_value_ready.shape[-1])
    input_back = (
        transposed_right(query_grad_low, full_query)
        + transposed_right(key_grad_low, full_key)
        + transposed_right(value_grad_low, full_value)
    )
    grad_input = grad_residual + reduce_rows(input_back.reshape(seqs_here, local_rows, model_width))
    grad_query_part = transposed_left(flat_in, query_grad_low)
    grad_key_part = transposed_left(flat_in, key_grad_low)
    grad_value_part = transposed_left(flat_in, value_grad_low)
    weight_parts = (
        grad_query_part,
        grad_key_part,
        grad_value_part,
        grad_output_part,
        grad_up_part,
        grad_gate_part,
        grad_down_part,
    )
    shares = (
        lax.psum_scatter(weight_parts[0], ("fsdp", "ctx"), scatter_dimension=0, tiled=True),
        lax.psum_scatter(weight_parts[1], ("fsdp", "ctx"), scatter_dimension=0, tiled=True),
        lax.psum_scatter(weight_parts[2], ("fsdp", "ctx"), scatter_dimension=0, tiled=True),
        lax.psum_scatter(weight_parts[3], ("fsdp", "ctx"), scatter_dimension=1, tiled=True),
        lax.psum_scatter(weight_parts[4], ("fsdp", "ctx"), scatter_dimension=0, tiled=True),
        lax.psum_scatter(weight_parts[5], ("fsdp", "ctx"), scatter_dimension=0, tiled=True),
        lax.psum_scatter(weight_parts[6], ("fsdp", "ctx"), scatter_dimension=1, tiled=True),
    )
    summed = (
        lax.all_gather(shares[0].astype(jnp.bfloat16), "ctx", axis=0, tiled=True).astype(
            jnp.float32
        ),
        lax.all_gather(shares[1].astype(jnp.bfloat16), "ctx", axis=0, tiled=True).astype(
            jnp.float32
        ),
        lax.all_gather(shares[2].astype(jnp.bfloat16), "ctx", axis=0, tiled=True).astype(
            jnp.float32
        ),
        lax.all_gather(shares[3].astype(jnp.bfloat16), "ctx", axis=1, tiled=True).astype(
            jnp.float32
        ),
        lax.all_gather(shares[4].astype(jnp.bfloat16), "ctx", axis=0, tiled=True).astype(
            jnp.float32
        ),
        lax.all_gather(shares[5].astype(jnp.bfloat16), "ctx", axis=0, tiled=True).astype(
            jnp.float32
        ),
        lax.all_gather(shares[6].astype(jnp.bfloat16), "ctx", axis=1, tiled=True).astype(
            jnp.float32
        ),
    )
    grad_query, grad_key, grad_value, grad_output, grad_up, grad_gate, grad_down = summed
    tensor_index = lax.axis_index("tp")

    def spread_slice(section, length):
        return lax.dynamic_update_slice_in_dim(
            jnp.zeros((length,), jnp.float32), section, tensor_index * section.shape[0], 0
        )

    grad_sharpness, grad_amplitude, grad_steepness, grad_attend, grad_mixer = lax.psum(
        (
            spread_slice(sharp_query + sharp_key, D),
            spread_slice(grad_amplitude_part, FF),
            spread_slice(grad_steepness_part, FF),
            grad_attend_part,
            grad_mixer_part,
        ),
        ("fsdp", "ctx", "tp"),
    )
    return (
        layer_out,
        grad_input,
        grad_query,
        grad_key,
        grad_value,
        grad_output,
        grad_sharpness,
        grad_attend,
        grad_up,
        grad_gate,
        grad_down,
        grad_amplitude,
        grad_steepness,
        grad_mixer,
    )


def solution(mesh):
    return jax.shard_map(
        per_device,
        mesh=mesh,
        in_specs=(
            P("fsdp", ("ctx", "tp"), None),
            P("fsdp", "tp"),
            P("fsdp", "tp"),
            P("fsdp", "tp"),
            P("tp", "fsdp"),
            P("tp"),
            P(),
            P("fsdp", "tp"),
            P("fsdp", "tp"),
            P("tp", "fsdp"),
            P("tp"),
            P("tp"),
            P(),
            P("fsdp", None),
            P("fsdp", "ctx"),
            P("fsdp", ("ctx", "tp"), None),
        ),
        out_specs=(
            P("fsdp", ("ctx", "tp"), None),
            P("fsdp", ("ctx", "tp"), None),
            P("fsdp", "tp"),
            P("fsdp", "tp"),
            P("fsdp", "tp"),
            P("tp", "fsdp"),
            P(),
            P(),
            P("fsdp", "tp"),
            P("fsdp", "tp"),
            P("tp", "fsdp"),
            P(),
            P(),
            P(),
        ),
        check_vma=False,
    )
```

profile of v0, /device:TPU:0, one launch (start us, length us, event | category | flops | bytes accessed | tf_op | source)
XLA Modules:
  0.0 1163.4 jit_solution(5434817711569213358)
XLA Ops:
  9.5 17.6 %all_gather.64 = bf16[1024,256]{1,0:T(8,128)(2,1)S(1)} all-gather(bf16[256,256]{1,0:T(8,128)(2,1)} %param.22), channel_id=1, replica_groups=mesh['fsdp'=4,'ctx'=2,'tp'=4] {'fsdp'}, dimensions={0}, use_global_device_ids=true | all-gather | bytes 655360 | tf_op jit(solution)/shard_map/all_gather | solution.py:98
  28.1 16.5 %all_gather.63 = bf16[1024,256]{1,0:T(8,128)(2,1)S(1)} all-gather(bf16[256,256]{1,0:T(8,128)(2,1)} %param.21), channel_id=1, replica_groups=mesh['fsdp'=4,'ctx'=2,'tp'=4] {'fsdp'}, dimensions={0}, use_global_device_ids=true | all-gather | bytes 655360 | tf_op jit(solution)/shard_map/all_gather | solution.py:97
  45.6 15.7 %all_gather.61 = bf16[1024,256]{1,0:T(8,128)(2,1)S(1)} all-gather(bf16[256,256]{1,0:T(8,128)(2,1)} %param.23), channel_id=1, replica_groups=mesh['fsdp'=4,'ctx'=2,'tp'=4] {'fsdp'}, dimensions={0}, use_global_device_ids=true | all-gather | bytes 655360 | tf_op jit(solution)/shard_map/all_gather | solution.py:99
  61.8 3.2 convolution_convert_fusion.1
  65.2 2.4 fusion.15
  72.7 14.8 %all_gather.66 = bf16[256,1024]{1,0:T(8,128)(2,1)S(1)} all-gather(bf16[256,256]{1,0:T(8,128)(2,1)S(1)} %copy-done.53), channel_id=1, replica_groups=mesh['fsdp'=4,'ctx'=2,'tp'=4] {'fsdp'}, dimensions={1}, use_global_device_ids=true | all-gather | bytes 655360 | tf_op jit(solution)/shard_map/all_gather | solution.py:100
  89.4 22.0 %all-gather.14.cloned.1.call-done = bf16[2,1024,256]{1,2,0:T(8,128)(2,1)} async-done(((bf16[2,512,256]{1,2,0:T(8,128)(2,1)}), bf16[2,1024,256]{1,2,0:T(8,128)(2,1)}) %all-gather.14.cloned.1.call-update) | async-done | bytes 1048592 | tf_op jit(solution)/shard_map/all_gather | solution.py:128
  111.4 17.2 %while.26 = (s32[]{:T(128)}, bf16[2,512,256]{1,2,0:T(8,128)(2,1)S(1)}, f32[2,4,512]{2,1,0:T(4,128)S(1)}, bf16[2,1024,256]{1,2,0:T(8,128)(2,1)S(1)}, s32[2,1024]{...) while((s32[]{:T(128)}, ...), condition=%wide.region_5.6_spmd, body=%wide.region_2.5_spmd.sunk | while | flops 562690048 | bytes 32065660 | solution.py:159
  114.6 2.3 fusion.115
  117.0 2.9 fusion.116
  123.2 2.3 fusion.115
  125.6 2.9 fusion.116
  129.4 2.7 fusion.27
  132.7 44.1 %reduce-scatter.14.cloned.1.call-done = f32[2,128,1024]{2,1,0:T(8,128)} async-done(((f32[2,512,1024]{2,1,0:T(8,128)}), f32[2,128,1024]{2,1,0:T(8,128)}) %reduce-scatter.14.cloned.1.call-update) | async-done | bytes 1048592 | tf_op jit(solution)/shard_map/reduce_scatter | solution.py:66
  182.5 20.9 %all-gather.16.cloned.1.call-done = bf16[2,512,1024]{2,1,0:T(8,128)(2,1)} async-done(((bf16[2,128,1024]{2,1,0:T(8,128)(2,1)}), bf16[2,512,1024]{2,1,0:T(8,128)(2,1)}) %all-gather.16.cloned.1.call-update) | async-done | bytes 2097168 | tf_op jit(solution)/shard_map/all_gather | solution.py:62
  203.4 6.6 fusion.38
  210.0 40.4 %all-gather.18.cloned.1.call-done = bf16[1024,1024]{1,0:T(8,128)(2,1)} async-done(((bf16[256,1024]{1,0:T(8,128)(2,1)}), bf16[1024,1024]{1,0:T(8,128)(2,1)}) %all-gather.18.cloned.1.call-update) | async-done | bytes 2097168 | tf_op jit(solution)/shard_map/all_gather | solution.py:101
  250.4 8.8 multiply_convert_fusion.3
  259.2 37.7 %all-gather.22.cloned.1.call-done = bf16[1024,1024]{1,0:T(8,128)(2,1)} async-done(((bf16[1024,256]{1,0:T(8,128)(2,1)}), bf16[1024,1024]{1,0:T(8,128)(2,1)}) %all-gather.22.cloned.1.call-update) | async-done | bytes 2097168 | tf_op jit(solution)/shard_map/all_gather | solution.py:103
  297.0 6.6 fusion.39
  303.7 42.7 %reduce-scatter.16.cloned.1.call-done = f32[2,128,1024]{2,1,0:T(8,128)} async-done(((f32[2,512,1024]{2,1,0:T(8,128)}), f32[2,128,1024]{2,1,0:T(8,128)}) %reduce-scatter.16.cloned.1.call-update) | async-done | bytes 1048592 | tf_op jit(solution)/shard_map/reduce_scatter | solution.py:66
  347.8 1.9 fusion.19
  351.4 2.4 fusion.20
  354.3 22.3 %all-gather.24.cloned.1.call-done = bf16[2,512,1024]{2,1,0:T(8,128)(2,1)} async-done(((bf16[2,128,1024]{2,1,0:T(8,128)(2,1)}), bf16[2,512,1024]{2,1,0:T(8,128)(2,1)}) %all-gather.24.cloned.1.call-update) | async-done | bytes 2097168 | tf_op jit(solution)/shard_map/all_gather | solution.py:62
  376.6 9.9 multiply_reduce_fusion.1
  386.5 2.4 fusion.40
  389.7 4.4 convolution_add_fusion
  394.1 44.7 %reduce-scatter.18.cloned.1.call-done = f32[2,128,1024]{2,1,0:T(8,128)} async-done(((f32[2,512,1024]{2,1,0:T(8,128)}), f32[2,128,1024]{2,1,0:T(8,128)}) %reduce-scatter.18.cloned.1.call-update) | async-done | bytes 1048592 | tf_op jit(solution)/shard_map/reduce_scatter | solution.py:66
  438.8 2.9 multiply_reduce_fusion.3
  441.7 3.7 multiply_reduce_fusion.4
  447.8 22.3 %all-gather.26.cloned.1.call-done = bf16[2,512,1024]{2,1,0:T(8,128)(2,1)} async-done(((bf16[2,128,1024]{2,1,0:T(8,128)(2,1)}), bf16[2,512,1024]{2,1,0:T(8,128)(2,1)}) %all-gather.26.cloned.1.call-update) | async-done | bytes 2097168 | tf_op jit(solution)/shard_map/all_gather | solution.py:62
  470.1 2.4 convolution_convert_fusion
  472.5 46.4 %while.27 = (s32[]{:T(128)}, f32[2,512,256]{1,2,0:T(8,128)}, bf16[2,1024,256]{1,2,0:T(8,128)(2,1)}, bf16[2,1024,256]{2,1,0:T(8,128)(2,1)}, bf16[2,1024,256]{1,2,...) while((s32[]{:T(128)}, f32[2,512,256]{1,2,0:T(8,128)}, ...), condition=%wide.region_19.20_spmd, body=%wide.region_17.19_spmd.sunk | while | flops 1374812160 | bytes 157886896 | solution.py:229
  476.7 3.5 fusion.128
  482.2 6.2 multiply_reduce_fusion.17
  488.4 2.4 multiply_convert_fusion.9
  499.9 3.5 fusion.128
  505.4 6.2 multiply_reduce_fusion.17
  511.6 2.4 multiply_convert_fusion.9
  519.7 6.6 fusion.44
  527.9 6.0 fusion.43
  534.0 6.5 fusion.26
  540.6 3.6 convolution_bitcast_fusion
  549.7 1.7 convolution_bitcast_fusion.3
  551.5 11.2 reduce-scatter.22.cloned.1.call-done
  562.7 2.8 convolution_bitcast_fusion.1
  571.7 2.8 add_add_fusion
  575.7 79.4 %reduce-scatter.38.cloned.1.call-done = f32[1024,128]{1,0:T(8,128)} async-done(((f32[1024,1024]{1,0:T(8,128)}), f32[1024,128]{1,0:T(8,128)}) %reduce-scatter.38.cloned.1.call-update) | async-done | bytes 524304 | tf_op jit(solution)/shard_map/reduce_scatter | solution.py:270
  656.2 8.5 all_gather.79
  665.7 80.8 %reduce-scatter.34.cloned.1.call-done = f32[128,1024]{1,0:T(8,128)} async-done(((f32[1024,1024]{1,0:T(8,128)}), f32[128,1024]{1,0:T(8,128)}) %reduce-scatter.34.cloned.1.call-update) | async-done | bytes 524304 | tf_op jit(solution)/shard_map/reduce_scatter | solution.py:268
  747.6 8.5 all_gather.77
  757.2 81.0 %reduce-scatter.36.cloned.1.call-done = f32[128,1024]{1,0:T(8,128)} async-done(((f32[1024,1024]{1,0:T(8,128)}), f32[128,1024]{1,0:T(8,128)}) %reduce-scatter.36.cloned.1.call-update) | async-done | bytes 524304 | tf_op jit(solution)/shard_map/reduce_scatter | solution.py:269
  839.3 8.3 all_gather.78
  850.1 55.7 %reduce-scatter.32.cloned.1.call-done = f32[256,128]{1,0:T(8,128)} async-done(((f32[256,1024]{1,0:T(8,128)}), f32[256,128]{1,0:T(8,128)}) %reduce-scatter.32.cloned.1.call-update) | async-done | bytes 131088 | tf_op jit(solution)/shard_map/reduce_scatter | solution.py:267
  906.7 5.0 all_gather.76
  913.8 41.2 %all-reduce.4 = (f32[1024]{0:T(1024)}, f32[1024]{0:T(1024)}, f32[4096]{0:T(1024)}, f32[4096]{0:T(1024)}, f32[1024]{0:T(1024)}) all-reduce(f32[1024]{0:T(1024)S(1)} %add_dynamic-update-slice_fusion, f32[1024]{0:T(1024)S(1)} %copy-done.58, ...), channel_id=1, replica_groups=mesh['fsdp'=4,'ctx'=2,'tp'=4] {'fsdp','ctx','tp'}, use_global_device_ids=true, to_apply=%region_31.32 | all-reduce | flops 11264 | bytes 90112 | tf_op jit(solution)/shard_map/psum | solution.py:303
  955.1 18.0 %reduce-scatter.26.cloned.1.call-done = f32[128,256]{0,1:T(8,128)} async-done(((f32[1024,256]{0,1:T(8,128)}), f32[128,256]{0,1:T(8,128)}) %reduce-scatter.26.cloned.1.call-update) | async-done | bytes 131088 | tf_op jit(solution)/shard_map/reduce_scatter | solution.py:264
  974.0 5.0 all_gather.73
  979.8 60.5 %reduce-scatter.30.cloned.1.call-done = f32[128,256]{0,1:T(8,128)} async-done(((f32[1024,256]{0,1:T(8,128)}), f32[128,256]{0,1:T(8,128)}) %reduce-scatter.30.cloned.1.call-update) | async-done | bytes 131088 | tf_op jit(solution)/shard_map/reduce_scatter | solution.py:266
  1041.2 5.0 all_gather.75
  1047.0 60.5 %reduce-scatter.28.cloned.1.call-done = f32[128,256]{0,1:T(8,128)} async-done(((f32[1024,256]{0,1:T(8,128)}), f32[128,256]{0,1:T(8,128)}) %reduce-scatter.28.cloned.1.call-update) | async-done | bytes 131088 | tf_op jit(solution)/shard_map/reduce_scatter | solution.py:265
  1108.4 5.0 all_gather.74
  1114.2 39.3 %reduce-scatter.24.cloned.1.call-done = f32[2,128,1024]{2,1,0:T(8,128)} async-done(((f32[2,512,1024]{2,1,0:T(8,128)}), f32[2,128,1024]{2,1,0:T(8,128)}) %reduce-scatter.24.cloned.1.call-update) | async-done | bytes 1048592 | tf_op jit(solution)/shard_map/reduce_scatter | solution.py:66
  1153.5 2.4 add_add_fusion.7
  (330 shorter events, 84.4 us)
Async XLA Ops:
  8.0 53.8 %all-gather.10.cloned.1.call-start = ((), (), s32[]{:S(2)}) async-start(), calls=%async_computation.13 | async-start | bytes 2621440 | tf_op jit(solution)/shard_map/all_gather | solution.py:62
  8.7 79.2 %all-gather.12.cloned.1.call-start = ((), (), s32[]{:S(2)}) async-start(), calls=%async_computation.14 | async-start | bytes 1572864 | tf_op jit(solution)/shard_map/all_gather | solution.py:129
  44.6 17.2 %copy-start.24 = (bf16[1024,256]{1,0:T(8,128)(2,1)}, bf16[1024,256]{1,0:T(8,128)(2,1)S(1)}, u32[]{:S(2)}) copy-start(bf16[1024,256]{1,0:T(8,128)(2,1)S(1)} %all_gather.63) | copy-start | bytes 1572868
  61.2 6.3 copy-start.35
  61.8 6.6 copy-start.37
  61.8 6.6 copy-start.39
  61.8 5.7 copy-start.3
  65.1 46.3 %all-gather.14.cloned.1.call-start = ((), (), s32[]{:S(2)}) async-start(), calls=%async_computation.15 | async-start | bytes 1572864 | tf_op jit(solution)/shard_map/all_gather | solution.py:128
  68.8 3.7 copy-start.7
  68.8 3.7 copy-start.9
  68.8 3.7 copy-start.11
  68.8 3.7 copy-start.13
  69.2 3.5 copy-start.44
  69.2 3.5 copy-start.53
  72.6 104.2 %reduce-scatter.14.cloned.1.call-start = ((), (), s32[]{:S(2)}) async-start(), calls=%async_computation.16 | async-start | bytes 5242880 | tf_op jit(solution)/shard_map/reduce_scatter | solution.py:66
  87.5 41.1 %copy-start.32 = (bf16[256,1024]{1,0:T(8,128)(2,1)}, bf16[256,1024]{1,0:T(8,128)(2,1)S(1)}, u32[]{:S(2)}) copy-start(bf16[256,1024]{1,0:T(8,128)(2,1)S(1)} %all_gather.66) | copy-start | bytes 1572868
  128.6 3.5 copy-start.5
  132.1 46.1 %copy-start.28 = (bf16[2,128,1024]{2,1,0:T(8,128)(2,1)S(1)}, bf16[2,128,1024]{2,1,0:T(8,128)(2,1)}, u32[]{:S(2)}) copy-start(bf16[2,128,1024]{2,1,0:T(8,128)(2,1)} %param.20) | copy-start | bytes 1572868
  132.1 46.1 %copy-start.55 = (f32[1024]{0:T(1024)S(1)}, f32[1024]{0:T(1024)}, u32[]{:S(2)}) copy-start(f32[1024]{0:T(1024)} %param.26) | copy-start | bytes 12292
  132.1 50.4 %all-gather.20.cloned.1.call-start = ((), (), s32[]{:S(2)}) async-start(), calls=%async_computation.19 | async-start | bytes 2621440 | tf_op jit(solution)/shard_map/all_gather | solution.py:102
  132.7 70.7 %all-gather.16.cloned.1.call-start = ((), (), s32[]{:S(2)}) async-start(), calls=%async_computation.17 | async-start | bytes 2621440 | tf_op jit(solution)/shard_map/all_gather | solution.py:62
  180.9 69.5 %all-gather.18.cloned.1.call-start = ((), (), s32[]{:S(2)}) async-start(), calls=%async_computation.18 | async-start | bytes 2621440 | tf_op jit(solution)/shard_map/all_gather | solution.py:101
  181.5 115.5 %all-gather.22.cloned.1.call-start = ((), (), s32[]{:S(2)}) async-start(), calls=%async_computation.20 | async-start | bytes 2621440 | tf_op jit(solution)/shard_map/all_gather | solution.py:103
  182.2 164.1 %reduce-scatter.16.cloned.1.call-start = ((), (), s32[]{:S(2)}) async-start(), calls=%async_computation.21 | async-start | bytes 5242880 | tf_op jit(solution)/shard_map/reduce_scatter | solution.py:66
  203.4 47.0 %copy-start.66 = (f32[1024]{0:T(1024)S(1)}, f32[1024]{0:T(1024)}, u32[]{:S(2)}) copy-start(f32[1024]{0:T(1024)} %param.30) | copy-start | bytes 12292
  203.4 47.0 %copy-start.67 = (f32[1024]{0:T(1024)S(1)}, f32[1024]{0:T(1024)}, u32[]{:S(2)}) copy-start(f32[1024]{0:T(1024)} %param.31) | copy-start | bytes 12292
  303.6 44.2 %copy-start.54 = (f32[1024]{0:T(1024)S(1)}, f32[1024]{0:T(1024)}, u32[]{:S(2)}) copy-start(f32[1024]{0:T(1024)} %param.32) | copy-start | bytes 12292
  303.6 73.0 %all-gather.24.cloned.1.call-start = ((), (), s32[]{:S(2)}) async-start(), calls=%async_computation.22 | async-start | bytes 2621440 | tf_op jit(solution)/shard_map/all_gather | solution.py:62
  353.9 84.9 %reduce-scatter.18.cloned.1.call-start = ((), (), s32[]{:S(2)}) async-start(), calls=%async_computation.23 | async-start | bytes 5242880 | tf_op jit(solution)/shard_map/reduce_scatter | solution.py:66
  376.6 9.9 copy-start.65
  394.1 76.0 %all-gather.26.cloned.1.call-start = ((), (), s32[]{:S(2)}) async-start(), calls=%async_computation.24 | async-start | bytes 2621440 | tf_op jit(solution)/shard_map/all_gather | solution.py:62
  447.5 96.8 %reduce-scatter.20.cloned.1.call-start = ((), (), s32[]{:S(2)}) async-start(), calls=%async_computation.25 | async-start | bytes 1572864 | tf_op jit(solution)/shard_map/reduce_scatter | solution.py:233
  472.8 3.9 copy-start.2
  476.6 3.5 copy-start
  481.4 7.0 slice-start
  482.2 6.2 slice-start.1
  495.9 3.9 copy-start.2
  504.6 7.0 slice-start
  505.4 6.2 slice-start.1
  518.9 43.8 %reduce-scatter.22.cloned.1.call-start = ((), (), s32[]{:S(2)}) async-start(), calls=%async_computation.26 | async-start | bytes 1572864 | tf_op jit(solution)/shard_map/reduce_scatter | solution.py:236
  519.7 135.4 %reduce-scatter.38.cloned.1.call-start = ((), (), s32[]{:S(2)}) async-start(), calls=%async_computation.34 | async-start | bytes 4718592 | tf_op jit(solution)/shard_map/reduce_scatter | solution.py:270
  526.3 220.2 %reduce-scatter.34.cloned.1.call-start = ((), (), s32[]{:S(2)}) async-start(), calls=%async_computation.32 | async-start | bytes 4718592 | tf_op jit(solution)/shard_map/reduce_scatter | solution.py:268
  533.9 304.3 %reduce-scatter.36.cloned.1.call-start = ((), (), s32[]{:S(2)}) async-start(), calls=%async_computation.33 | async-start | bytes 4718592 | tf_op jit(solution)/shard_map/reduce_scatter | solution.py:269
  540.5 3.8 copy-start.60
  540.5 3.9 copy-start.8
  540.5 3.9 copy-start.10
  540.5 3.9 copy-start.12
  540.5 3.9 copy-start.14
  540.5 3.9 copy-start.23
  540.5 5.4 copy-start.52
  540.5 5.4 copy-start.50
  540.6 5.4 copy-start.46
  540.6 5.4 copy-start.48
  540.6 365.2 %reduce-scatter.32.cloned.1.call-start = ((), (), s32[]{:S(2)}) async-start(), calls=%async_computation.31 | async-start | bytes 1179648 | tf_op jit(solution)/shard_map/reduce_scatter | solution.py:267
  544.2 428.9 %reduce-scatter.26.cloned.1.call-start = ((), (), s32[]{:S(2)}) async-start(), calls=%async_computation.28 | async-start | bytes 1179648 | tf_op jit(solution)/shard_map/reduce_scatter | solution.py:264
  551.5 488.8 %reduce-scatter.30.cloned.1.call-start = ((), (), s32[]{:S(2)}) async-start(), calls=%async_computation.30 | async-start | bytes 1179648 | tf_op jit(solution)/shard_map/reduce_scatter | solution.py:266
  565.5 542.0 %reduce-scatter.28.cloned.1.call-start = ((), (), s32[]{:S(2)}) async-start(), calls=%async_computation.29 | async-start | bytes 1179648 | tf_op jit(solution)/shard_map/reduce_scatter | solution.py:265
  568.6 584.9 %reduce-scatter.24.cloned.1.call-start = ((), (), s32[]{:S(2)}) async-start(), calls=%async_computation.27 | async-start | bytes 5242880 | tf_op jit(solution)/shard_map/reduce_scatter | solution.py:66
  656.2 192.5 %copy-start.18 = (f32[2,512,4,64]{1,3,2,0:T(8,128)S(1)}, f32[2,512,4,64]{1,3,2,0:T(8,128)}, u32[]{:S(2)}) copy-start(f32[2,512,4,64]{1,3,2,0:T(8,128)} %copy-done.17) | copy-start | bytes 3145732
  747.6 164.8 %copy-start.16 = (f32[2,512,4,64]{1,3,2,0:T(8,128)S(1)}, f32[2,512,4,64]{1,3,2,0:T(8,128)}, u32[]{:S(2)}) copy-start(f32[2,512,4,64]{1,3,2,0:T(8,128)} %copy-done.15) | copy-start | bytes 3145732
  757.2 156.6 %copy-start.57 = (f32[1024]{0:T(1024)S(1)}, f32[1024]{0:T(1024)}, u32[]{:S(2)}) copy-start(f32[1024]{0:T(1024)} %get-tuple-element.189) | copy-start | bytes 12292
  757.2 156.6 %copy-start.58 = (f32[1024]{0:T(1024)S(1)}, f32[1024]{0:T(1024)}, u32[]{:S(2)}) copy-start(f32[1024]{0:T(1024)} %get-tuple-element.193) | copy-start | bytes 12292
  847.6 305.9 %copy-start.20 = (f32[2,128,1024]{2,1,0:T(8,128)S(1)}, f32[2,128,1024]{2,1,0:T(8,128)}, u32[]{:S(2)}) copy-start(f32[2,128,1024]{2,1,0:T(8,128)} %copy-done.19) | copy-start | bytes 3145732
  847.6 305.9 %copy-start.56 = (f32[1024]{0:T(1024)S(1)}, f32[1024]{0:T(1024)}, u32[]{:S(2)}) copy-start(f32[1024]{0:T(1024)} %param.26) | copy-start | bytes 12292
  (40 other events, 78.5 us)
Sparse Core Ops, SparseCore 0:
  10.4 25.2 all-gather.9
  65.2 22.6 all-gather.11
  90.1 21.2 all-gather.13
  132.2 44.5 reduce-scatter.13
  354.0 22.5 all-gather.23
  394.2 44.5 reduce-scatter.17
  519.1 20.3 reduce-scatter.19
  542.3 20.3 reduce-scatter.21
  566.4 88.6 reduce-scatter.37
  658.6 87.9 reduce-scatter.33
  750.2 87.9 reduce-scatter.35
  841.5 64.2 reduce-scatter.31
  909.2 63.8 reduce-scatter.25
  976.4 63.9 reduce-scatter.29
  1043.6 63.8 reduce-scatter.27
  1109.9 43.5 reduce-scatter.23
Sparse Core Ops, SparseCore 1:
  134.2 45.5 all-gather.19
  181.7 21.7 all-gather.15
  204.9 45.5 all-gather.17
  252.0 44.9 all-gather.21
  303.7 42.6 reduce-scatter.15
  447.6 22.4 all-gather.25
where the time goes:
time: 1170 us; the launch traced here: 1160 us
  waiting for transfers between devices  788 us (67%)
  blocking collectives  151 us (13%)
  matrix products  119 us (10%)
  other arithmetic  55.1 us (5%)
  local copies, waits for them, and re-layouts  31.6 us (3%)
  between operations  16.8 us (1%)
    reduce_scatter x4, waiting for transfers between devices, reduce_rows(): return lax.psum_scatter(values, 'tp', scatter_dimension=1, tiled=True)  171 us
    reduce_scatter x1, waiting for transfers between devices, per_device(): lax.psum_scatter(weight_parts[5], ('fsdp', 'ctx'), scatter_dimension=0, t...  81 us
    reduce_scatter x1, waiting for transfers between devices, per_device(): lax.psum_scatter(weight_parts[4], ('fsdp', 'ctx'), scatter_dimension=0, t...  80.8 us
    reduce_scatter x1, waiting for transfers between devices, per_device(): lax.psum_scatter(weight_parts[6], ('fsdp', 'ctx'), scatter_dimension=1, t...  79.4 us
    all_gather x4, waiting for transfers between devices, gather_rows(): return lax.all_gather(values, 'tp', axis=1, tiled=True)  65.5 us
    reduce_scatter x1, waiting for transfers between devices, per_device(): lax.psum_scatter(weight_parts[2], ('fsdp', 'ctx'), scatter_dimension=0, t...  60.5 us
    reduce_scatter x1, waiting for transfers between devices, per_device(): lax.psum_scatter(weight_parts[1], ('fsdp', 'ctx'), scatter_dimension=0, t...  60.5 us
    reduce_scatter x1, waiting for transfers between devices, per_device(): lax.psum_scatter(weight_parts[3], ('fsdp', 'ctx'), scatter_dimension=1, t...  55.7 us
  transfers between devices with their start and end apart: 22, of which 19 were waited for; matrix products, arithmetic and copies ran while one was open for 7% of the time, Pallas kernels for 0%

commit v1 on v0

v1 whole, which is shorter than its diff:
```python
import math

import jax
import jax.numpy as jnp
from jax import lax
from jax.sharding import PartitionSpec as P

HD = 64
norm_eps = 1e-06
rope_base = 10000.0
BF = jnp.bfloat16
F32 = jnp.float32


def unit_rows(values):
    return values * lax.rsqrt(jnp.mean(values * values, axis=-1, keepdims=True) + norm_eps)


def rotate_pairs(values, angles):
    middle = values.shape[-1] // 2
    leading = values[..., :middle]
    trailing = values[..., middle:]
    cosine = jnp.cos(angles)[..., None, :]
    sine_part = jnp.sin(angles)[..., None, :]
    return jnp.concatenate(
        [leading * cosine - trailing * sine_part, trailing * cosine + leading * sine_part], axis=-1
    )


def angles_for(positions, head_size):
    middle = head_size // 2
    frequency = rope_base ** (-2.0 * jnp.arange(middle).astype(F32) / head_size)
    return positions.astype(F32)[..., None] * frequency


def prepare_heads(projected, angles, gains, head_size):
    heads_here = projected.shape[-1] // head_size
    shaped = projected.reshape(projected.shape[:-1] + (heads_here, head_size))
    normed = unit_rows(rotate_pairs(shaped, angles)) * gains.reshape(heads_here, head_size)
    return normed.reshape(projected.shape)


def product(left, right):
    return jnp.dot(left, right, preferred_element_type=F32)


def transposed_left(left, right):
    return lax.dot_general(left, right, (((0,), (0,)), ((), ())), preferred_element_type=F32)


def transposed_right(left, right):
    return lax.dot_general(left, right, (((1,), (1,)), ((), ())), preferred_element_type=F32)


def gather_rows(values):
    return lax.all_gather(values, "tp", axis=1, tiled=True)


def reduce_rows(values):
    return lax.psum_scatter(values.astype(BF), "tp", scatter_dimension=1, tiled=True).astype(F32)


def branch_mix(branch, base, rate):
    return unit_rows(base + rate * (unit_rows(branch) - base))


def activate(upper, gated_raw, amplitude, steepness):
    scaled = gated_raw * steepness
    return upper * amplitude * (scaled * jax.nn.sigmoid(scaled))


def trade(values, sizes):
    n = sizes["ctx"]
    me = lax.axis_index("ctx")
    if n == 2:
        own = lax.dynamic_index_in_dim(values, me, 0, keepdims=False)
        other = lax.dynamic_index_in_dim(values, 1 - me, 0, keepdims=False)
        got = lax.ppermute(other, "ctx", [(0, 1), (1, 0)])
        first = jnp.where(me == 0, own, got)
        second = jnp.where(me == 0, got, own)
        return jnp.stack([first, second])
    return lax.all_to_all(values, "ctx", split_axis=0, concat_axis=0, tiled=True)


def attend_both(query_low, key_low, value_low, ids):
    length, width = query_low.shape
    heads = width // HD
    q = query_low.reshape(length, heads, HD)
    k = key_low.reshape(length, heads, HD)
    v = value_low.reshape(length, heads, HD)
    scores = jnp.einsum("qhd,khd->hqk", q, k, preferred_element_type=F32) / math.sqrt(HD)
    allowed = ids[None, :] <= ids[:, None]
    scores = jnp.where(allowed[None], scores, -1e30)
    row_max = jnp.max(scores, axis=-1, keepdims=True)
    exponent = jnp.exp(scores - row_max)
    row_total = jnp.sum(exponent, axis=-1, keepdims=True)
    weights_low = (exponent / row_total).astype(BF)
    out = jnp.einsum("hqk,khd->qhd", weights_low, v, preferred_element_type=F32)
    return out.reshape(length, width).astype(BF), (row_max + jnp.log(row_total))[..., 0]


def attend_back(query_low, key_low, value_low, ids, logsum, grad):
    length, width = query_low.shape
    heads = width // HD
    q = query_low.reshape(length, heads, HD)
    k = key_low.reshape(length, heads, HD)
    v = value_low.reshape(length, heads, HD)
    g = grad.reshape(length, heads, HD)
    scores = jnp.einsum("qhd,khd->hqk", q, k, preferred_element_type=F32) / math.sqrt(HD)
    allowed = ids[None, :] <= ids[:, None]
    scores = jnp.where(allowed[None], scores, -1e30)
    soft = jnp.exp(scores - logsum[..., None])
    grad_v = jnp.einsum("hqk,qhd->khd", soft.astype(BF), g, preferred_element_type=F32)
    grad_w = jnp.einsum("qhd,khd->hqk", g, v, preferred_element_type=F32)
    grad_s = soft * (grad_w - jnp.sum(grad_w * soft, axis=-1, keepdims=True))
    low = grad_s.astype(BF)
    grad_q = jnp.einsum("hqk,khd->qhd", low, k, preferred_element_type=F32) / math.sqrt(HD)
    grad_k = jnp.einsum("hqk,qhd->khd", low, q, preferred_element_type=F32) / math.sqrt(HD)
    return (
        grad_q.reshape(length, width),
        grad_k.reshape(length, width),
        grad_v.reshape(length, width),
    )


def per_device(sizes):
    def run(
        residual,
        query_weight,
        key_weight,
        value_weight,
        output_weight,
        sharpness,
        attend_rate,
        up_weight,
        gate_weight,
        down_weight,
        amplitude,
        steepness,
        mixer_rate,
        block_ids,
        positions,
        cotangent,
    ):
        z = sizes["fsdp"]
        width = residual.shape[2]
        hidden_here = up_weight.shape[1]
        heads_width = query_weight.shape[1]

        mine = trade(residual, sizes)
        qkv_shard = jnp.concatenate([query_weight, key_weight, value_weight], axis=1)
        full_qkv = lax.all_gather(qkv_shard, "fsdp", axis=0, tiled=True)
        full_output = lax.all_gather(output_weight, "fsdp", axis=1, tiled=True)
        ug_shard = jnp.concatenate([up_weight, gate_weight], axis=1)
        full_ug = lax.all_gather(ug_shard, "fsdp", axis=0, tiled=True)
        full_down = lax.all_gather(down_weight, "fsdp", axis=1, tiled=True)

        ctx = lax.axis_index("ctx")
        ids = lax.dynamic_index_in_dim(block_ids, ctx, 0, keepdims=False)
        all_positions = lax.all_gather(positions, "ctx", axis=1, tiled=True)
        my_positions = lax.dynamic_index_in_dim(all_positions, ctx, 0, keepdims=False)
        angles = angles_for(my_positions, HD)

        gathered = gather_rows(mine)
        shape3 = gathered.shape
        flat_in = gathered.reshape(-1, width)
        raw = product(flat_in, full_qkv)
        raw_query, raw_key, raw_value = jnp.split(raw, 3, axis=1)

        def prepare_local(projected, gains):
            return prepare_heads(projected, angles, gains, HD)

        query_ready, query_back = jax.vjp(prepare_local, raw_query, sharpness)
        key_ready, key_back = jax.vjp(prepare_local, raw_key, sharpness)
        query_low = query_ready.astype(BF)
        key_low = key_ready.astype(BF)
        value_low = raw_value.astype(BF)
        attended, logsum = attend_both(query_low, key_low, value_low, ids)
        attend_sum = reduce_rows(product(attended, full_output).reshape(shape3))
        residual_float = mine.astype(F32)
        first, attend_back_mix = jax.vjp(branch_mix, attend_sum, residual_float, attend_rate)
        first_all = gather_rows(first.astype(BF)).reshape(-1, width)
        ug_raw = product(first_all, full_ug)
        up_raw, gate_raw = ug_raw[:, :hidden_here], ug_raw[:, hidden_here:]
        hidden, activate_back = jax.vjp(activate, up_raw, gate_raw, amplitude, steepness)
        hidden_low = hidden.astype(BF)
        down_sum = reduce_rows(product(hidden_low, full_down).reshape(shape3))
        outcome, mixer_back = jax.vjp(branch_mix, down_sum, first, mixer_rate)
        layer_out = trade(outcome.astype(BF), sizes)
        my_cot = trade(cotangent, sizes)
        grad_down_sum, grad_first, grad_mixer_part = mixer_back(my_cot.astype(F32))
        down_grad_all = gather_rows(grad_down_sum.astype(BF)).reshape(-1, width)
        grad_hidden = transposed_right(down_grad_all, full_down)
        grad_down_part = transposed_left(hidden_low, down_grad_all)
        grad_up_raw, grad_gate_raw, grad_amplitude_part, grad_steepness_part = activate_back(
            grad_hidden
        )
        ug_grad = jnp.concatenate([grad_up_raw.astype(BF), grad_gate_raw.astype(BF)], axis=1)
        first_back = transposed_right(ug_grad, full_ug)
        grad_first = grad_first + reduce_rows(first_back.reshape(shape3))
        grad_ug_part = transposed_left(first_all, ug_grad)
        grad_attend_sum, grad_residual, grad_attend_part = attend_back_mix(grad_first)
        attend_grad_all = gather_rows(grad_attend_sum.astype(BF)).reshape(-1, width)
        grad_output_part = transposed_left(attended, attend_grad_all)
        grad_attended = transposed_right(attend_grad_all, full_output).astype(BF)
        grad_query_ready, grad_key_ready, grad_value_ready = attend_back(
            query_low, key_low, value_low, ids, logsum, grad_attended
        )
        grad_raw_query, sharp_query = query_back(grad_query_ready)
        grad_raw_key, sharp_key = key_back(grad_key_ready)
        qkv_grad = jnp.concatenate(
            [grad_raw_query.astype(BF), grad_raw_key.astype(BF), grad_value_ready.astype(BF)], axis=1
        )
        input_back = transposed_right(qkv_grad, full_qkv)
        grad_input = grad_residual + reduce_rows(input_back.reshape(shape3))
        grad_input = trade(grad_input.astype(BF), sizes).astype(F32)
        grad_qkv_part = transposed_left(flat_in, qkv_grad)

        def sum_rows(part):
            share = lax.psum_scatter(
                part.astype(BF), ("fsdp", "ctx"), scatter_dimension=0, tiled=True
            )
            return lax.all_gather(share, "ctx", axis=0, tiled=True).astype(F32)

        def sum_columns(part):
            share = lax.psum_scatter(
                part.astype(BF), ("fsdp", "ctx"), scatter_dimension=1, tiled=True
            )
            return lax.all_gather(share, "ctx", axis=1, tiled=True).astype(F32)

        grad_down = sum_columns(grad_down_part)
        grad_ug = sum_rows(grad_ug_part)
        grad_output = sum_columns(grad_output_part)
        grad_qkv = sum_rows(grad_qkv_part)
        grad_up, grad_gate = grad_ug[:, :hidden_here], grad_ug[:, hidden_here:]
        grad_query, grad_key, grad_value = jnp.split(grad_qkv, 3, axis=1)
        tensor_index = lax.axis_index("tp")
        tp = sizes["tp"]

        def spread_slice(section):
            return lax.dynamic_update_slice_in_dim(
                jnp.zeros((section.shape[0] * tp,), F32),
                section,
                tensor_index * section.shape[0],
                0,
            )

        grad_sharpness, grad_amplitude, grad_steepness, grad_attend, grad_mixer = lax.psum(
            (
                spread_slice(sharp_query + sharp_key),
                spread_slice(grad_amplitude_part),
                spread_slice(grad_steepness_part),
                grad_attend_part,
                grad_mixer_part,
            ),
            ("fsdp", "ctx", "tp"),
        )
        return (
            layer_out,
            grad_input,
            grad_query,
            grad_key,
            grad_value,
            grad_output,
            grad_sharpness,
            grad_attend,
            grad_up,
            grad_gate,
            grad_down,
            grad_amplitude,
            grad_steepness,
            grad_mixer,
        )

    return run


def solution(mesh):
    return jax.shard_map(
        per_device(dict(mesh.shape)),
        mesh=mesh,
        in_specs=(
            P("fsdp", ("ctx", "tp"), None),
            P("fsdp", "tp"),
            P("fsdp", "tp"),
            P("fsdp", "tp"),
            P("tp", "fsdp"),
            P("tp"),
            P(),
            P("fsdp", "tp"),
            P("fsdp", "tp"),
            P("tp", "fsdp"),
            P("tp"),
            P("tp"),
            P(),
            P("fsdp", None),
            P("fsdp", "ctx"),
            P("fsdp", ("ctx", "tp"), None),
        ),
        out_specs=(
            P("fsdp", ("ctx", "tp"), None),
            P("fsdp", ("ctx", "tp"), None),
            P("fsdp", "tp"),
            P("fsdp", "tp"),
            P("fsdp", "tp"),
            P("tp", "fsdp"),
            P(),
            P(),
            P("fsdp", "tp"),
            P("fsdp", "tp"),
            P("tp", "fsdp"),
            P(),
            P(),
            P(),
        ),
        check_vma=False,
    )
```

time: 1170 us -> 824 us (0.70)
  waiting for transfers between devices: 788 us -> 508 us
  blocking collectives: 151 us -> 87.2 us
    reduce_scatter x13 -> x6, waiting for transfers between devices: 618 us -> 223 us  [the longest x2 112 us: sum_rows(): lax.psum_scatter(part.astype(BF), ('fsdp', 'ctx'), scatter_dimension=0, t...]
    all_gather x11 -> x5, blocking collectives: 110 us -> 46.4 us  [the longest x1 23.3 us: run(): full_output = lax.all_gather(output_weight, 'fsdp', axis=1, tiled=True)]
    unnamed x22 -> x18, waiting for transfers between devices: 3.38 us -> 58.8 us
    all_gather x5 -> x4, waiting for transfers between devices: 101 us -> 134 us  [the longest x1 76.5 us: run(): full_ug = lax.all_gather(ug_shard, 'fsdp', axis=0, tiled=True)]
    ppermute x0 -> x4, waiting for transfers between devices: none -> 21 us  [trade(): got = lax.ppermute(other, 'ctx', [(0, 1), (1, 0)])]
    dot_general x7 -> x4, matrix products: 28.8 us -> 21.9 us  [transposed_left(): lax.dot_general(left, right, (((0,), (0,)), ((), ())), preferred_element_...]
    dot_general x21 -> x10, matrix products: 66.7 us -> 66.2 us  [the longest x4 18.8 us: product(): return jnp.dot(left, right, preferred_element_type=F32)]
  transfers between devices with their start and end apart: 22 -> 20, of which waited for: 19 -> 19; matrix products, arithmetic and copies ran while one was open for 7% -> 14% of each run, Pallas kernels for 0% -> 0%
where the time goes in v1:
time: 824 us; the launch traced here: 815 us
  waiting for transfers between devices  508 us (62%)
  matrix products  109 us (13%)
  blocking collectives  87.2 us (11%)
  other arithmetic  58.8 us (7%)
  local copies, waits for them, and re-layouts  27.1 us (3%)
  between operations  15.2 us (2%)
  starting transfers between devices  9.4 us (1%)
    reduce_scatter x2, waiting for transfers between devices, sum_rows(): lax.psum_scatter(part.astype(BF), ('fsdp', 'ctx'), scatter_dimension=0, t...  112 us
    reduce_scatter x4, waiting for transfers between devices, reduce_rows(): lax.psum_scatter(values.astype(BF), 'tp', scatter_dimension=1, tiled=True)  111 us
    all_gather x1, waiting for transfers between devices, run(): full_ug = lax.all_gather(ug_shard, 'fsdp', axis=0, tiled=True)  76.5 us
    all_gather x4, waiting for transfers between devices, gather_rows(): return lax.all_gather(values, 'tp', axis=1, tiled=True)  71.7 us
    unnamed x18, waiting for transfers between devices  58.8 us
    psum x1, blocking collectives, run(): lax.psum((spread_slice(sharp_query + sharp_key), spread_slice(grad_amplit...  40.8 us
    all_gather x1, waiting for transfers between devices, run(): full_down = lax.all_gather(down_weight, 'fsdp', axis=1, tiled=True)  35.1 us
    all_gather x1, blocking collectives, run(): full_output = lax.all_gather(output_weight, 'fsdp', axis=1, tiled=True)  23.3 us
  transfers between devices with their start and end apart: 20, of which 19 were waited for; matrix products, arithmetic and copies ran while one was open for 14% of the time, Pallas kernels for 0%

profile of v1, /device:TPU:0, one launch (start us, length us, event | category | flops | bytes accessed | tf_op | source)
XLA Modules:
  0.0 815.2 jit_solution(5183301861423763717)
XLA Ops:
  7.3 1.8 pad_maximum_fusion.14
  10.2 3.0 collective-permute-start
  13.2 6.3 collective-permute-done
  21.6 4.3 all_gather.41
  25.9 23.3 %all_gather.42 = bf16[256,1024]{1,0:T(8,128)(2,1)S(1)} all-gather(bf16[256,256]{1,0:T(8,128)(2,1)S(1)} %copy-done.32), channel_id=1, replica_groups=mesh['fsdp'=4,'ctx'=2,'tp'=4] {'fsdp'}, dimensions={1}, use_global_device_ids=true | all-gather | bytes 655360 | tf_op jit(solution)/shard_map/all_gather | solution.py:153
  49.8 1.6 broadcast_compare_fusion
  51.4 7.0 all-gather.11.cloned.1.call-done
  58.4 23.6 %all-gather.9.cloned.1.call-done = bf16[2,512,1024]{2,1,0:T(8,128)(2,1)} async-done(((bf16[2,128,1024]{2,1,0:T(8,128)(2,1)}), bf16[2,512,1024]{2,1,0:T(8,128)(2,1)}) %all-gather.9.cloned.1.call-update) | async-done | bytes 2097168 | tf_op jit(solution)/shard_map/all_gather | solution.py:56
  82.0 3.9 fusion.54
  87.5 7.7 fusion.53
  95.2 8.0 fusion
  103.2 8.2 %fusion.14 = bf16[4,64,1024]{2,1,0:T(8,128)(2,1)} fusion(bf16[1024,4,64]{0,2,1:T(8,128)(2,1)S(1)} %bitcast.135, f32[4,1024,1024]{1,2,0:T(8,128)} %get-tuple-element.74, f32[4,1024]{1,0:T(4,128)S(1)} %fusion, f32[4,1024]{1,0:T(4,128)S(1)} %get-tuple-element.73), kind=kOutput, calls=%fused_computation.55 | convolution fusion | flops 549715968 | bytes 17858560 | tf_op jit(solution)/shard_map/hqk,khd->qhd/dot_general | solution.py:98
  112.8 2.1 convolution_convert_fusion.3
  115.0 2.3 pad_maximum_fusion.8
  117.8 28.4 %reduce-scatter.13.cloned.1.call-done = bf16[2,128,1024]{2,1,0:T(8,128)(2,1)} async-done(((bf16[2,512,1024]{2,1,0:T(8,128)(2,1)}), bf16[2,128,1024]{2,1,0:T(8,128)(2,1)}) %reduce-scatter.13.cloned.1.call-update) | async-done | bytes 524304 | tf_op jit(solution)/shard_map/reduce_scatter | solution.py:60
  149.6 2.2 multiply_convert_fusion.7
  152.5 76.5 %all-gather.15.cloned.1.call-done = bf16[1024,2048]{1,0:T(8,128)(2,1)} async-done(((bf16[256,2048]{1,0:T(8,128)(2,1)}), bf16[1024,2048]{1,0:T(8,128)(2,1)}) %all-gather.15.cloned.1.call-update) | async-done | bytes 4194320 | tf_op jit(solution)/shard_map/all_gather | solution.py:155
  229.0 23.1 %all-gather.13.cloned.1.call-done = bf16[2,512,1024]{2,1,0:T(8,128)(2,1)} async-done(((bf16[2,128,1024]{2,1,0:T(8,128)(2,1)}), bf16[2,512,1024]{2,1,0:T(8,128)(2,1)}) %all-gather.13.cloned.1.call-update) | async-done | bytes 2097168 | tf_op jit(solution)/shard_map/all_gather | solution.py:56
  252.1 6.9 fusion.55
  259.1 3.3 copy-done.9
  262.3 2.3 multiply_convert_fusion.3
  264.7 35.1 %all-gather.17.cloned.1.call-done = bf16[1024,1024]{1,0:T(8,128)(2,1)} async-done(((bf16[1024,256]{1,0:T(8,128)(2,1)}), bf16[1024,1024]{1,0:T(8,128)(2,1)}) %all-gather.17.cloned.1.call-update) | async-done | bytes 2097168 | tf_op jit(solution)/shard_map/all_gather | solution.py:156
  299.8 5.9 convolution_convert_fusion.2
  305.8 1.5 collective-permute-start.2
  307.3 6.4 collective-permute-done.2
  314.7 20.5 %reduce-scatter.15.cloned.1.call-done = bf16[2,128,1024]{2,1,0:T(8,128)(2,1)} async-done(((bf16[2,512,1024]{2,1,0:T(8,128)(2,1)}), bf16[2,128,1024]{2,1,0:T(8,128)(2,1)}) %reduce-scatter.15.cloned.1.call-update) | async-done | bytes 524304 | tf_op jit(solution)/shard_map/reduce_scatter | solution.py:60
  336.5 1.9 fusion.15
  338.5 2.4 fusion.22
  340.9 1.8 fusion.16
  343.0 22.5 %all-gather.19.cloned.1.call-done = bf16[2,512,1024]{2,1,0:T(8,128)(2,1)} async-done(((bf16[2,128,1024]{2,1,0:T(8,128)(2,1)}), bf16[2,512,1024]{2,1,0:T(8,128)(2,1)}) %all-gather.19.cloned.1.call-update) | async-done | bytes 2097168 | tf_op jit(solution)/shard_map/all_gather | solution.py:56
  365.5 9.4 %multiply_reduce_fusion.1 = (f32[1024]{0:T(1024)}, f32[1024]{0:T(1024)}, f32[1024,1024]{1,0:T(8,128)S(1)}, bf16[1024,1024]{1,0:T(8,128)(2,1)S(1)}) fusion(f32[1024,2048]{1,0:T(8,128)} %copy-done.9, f32[1024]{0:T(1024)} %param.27, f32[1024]{0:T(1024)} %param.26, bf16[1024,1024]{1,0:T(8,128)(2,1)} %bitcast.157, ...), kind=kOutput, calls=%fused_computation.15 | convolution fusion | flops 2168453120 | bytes 18890752 | tf_op jit(solution)/shard_map/dot_general | solution.py:52
  375.5 3.1 copy-done.56
  378.6 5.8 fusion.10
  384.4 31.3 %reduce-scatter.17.cloned.1.call-done = bf16[2,128,1024]{2,1,0:T(8,128)(2,1)} async-done(((bf16[2,512,1024]{2,1,0:T(8,128)(2,1)}), bf16[2,128,1024]{2,1,0:T(8,128)(2,1)}) %reduce-scatter.17.cloned.1.call-update) | async-done | bytes 524304 | tf_op jit(solution)/shard_map/reduce_scatter | solution.py:60
  415.7 2.8 multiply_reduce_fusion.3
  419.2 2.7 multiply_reduce_fusion.4
  424.0 9.4 %convolution_convert_fusion = bf16[1024,2048]{1,0:T(8,128)(2,1)} fusion(bf16[1024,1024]{1,0:T(8,128)(2,1)} %bitcast.156, bf16[1024,1024]{1,0:T(8,128)(2,1)} %copy-done.18, bf16[1024,1024]{1,0:T(8,128)(2,1)} %copy-done.59), kind=kOutput, calls=%fused_computation.24 | convolution fusion | flops 4305453056 | bytes 10485760 | tf_op jit(solution)/shard_map/dot_general | solution.py:48
  434.2 5.9 convolution_convert_fusion.1
  440.1 4.0 copy.46
  444.2 2.5 all-gather.21.cloned.1.call-done
  446.7 2.5 convolution_convert_fusion.7
  449.2 1.9 convolution_convert_fusion.6
  452.2 13.7 %multiply_reduce_fusion = (f32[4,1024]{1,0:T(4,128)S(1)}, f32[4,1024,1024]{1,2,0:T(8,128)}) fusion(f32[4,1024,1024]{1,2,0:T(8,128)} %get-tuple-element.74, f32[4,1024]{1,0:T(4,128)S(1)} %log_add_fusion, bf16[1024,4,64]{0,2,1:T(8,128)(2,1)S(1)} %bitcast.133, bf16[1024,4,64]{0,2,1:T(8,128)(2,1)} %bitcast.136), kind=kOutput, calls=%fused_computation.1 | convolution fusion | flops 549449728 | bytes 34635776 | tf_op jit(solution)/shard_map/qhd,khd->hqk/dot_general | solution.py:114
  469.4 10.9 %multiply_convert_fusion = bf16[4,1024,1024]{1,2,0:T(8,128)(2,1)} fusion(f32[4,1024,1024]{1,2,0:T(8,128)} %get-tuple-element.76, f32[4,1024,1024]{1,2,0:T(8,128)S(1)} %bitcast.129, f32[4,1024]{1,0:T(4,128)S(1)} %get-tuple-element.75, f32[4,1024]{1,0:T(4,128)S(1)} %log_add_fusion), kind=kLoop, calls=%fused_computation | loop fusion | flops 16777216 | bytes 41975808 | tf_op jit(solution)/shard_map/convert_element_type | solution.py:116
  480.3 6.2 fusion.47
  486.6 3.1 fusion.24
  489.9 2.1 add_add_fusion.1
  492.4 46.2 %reduce-scatter.23.cloned.1.call-done = bf16[128,2048]{1,0:T(8,128)(2,1)} async-done(((bf16[1024,2048]{1,0:T(8,128)(2,1)}), bf16[128,2048]{1,0:T(8,128)(2,1)}) %reduce-scatter.23.cloned.1.call-update) | async-done | bytes 524304 | tf_op jit(solution)/shard_map/reduce_scatter | solution.py:220
  539.0 8.6 %fusion.11 = bf16[4,64,1024]{2,1,0:T(8,128)(2,1)S(1)} fusion(bf16[1024,4,64]{0,2,1:T(8,128)(2,1)S(1)} %bitcast.134, f32[4,1024,1024]{1,2,0:T(8,128)} %get-tuple-element.74, f32[4,1024]{1,0:T(4,128)S(1)} %log_add_fusion), kind=kOutput, calls=%fused_computation.52 | convolution fusion | flops 545521664 | bytes 17842176 | tf_op jit(solution)/shard_map/hqk,qhd->khd/dot_general | solution.py:113
  547.6 3.2 convolution_convert_fusion.4
  550.9 4.6 convolution_convert_fusion.5
  555.6 1.5 collective-permute-start.1
  557.1 8.3 %collective-permute-done.1 = bf16[128,1024]{1,0:T(8,128)(2,1)S(1)} collective-permute-done((bf16[128,1024]{1,0:T(8,128)(2,1)S(1)}, bf16[128,1024]{1,0:T(8,128)(2,1)S(1)}, u32[]{:S(2)}, u32[]{:S(2)}) %collective-permute-start.1) | collective-permute-done | bytes 262176 | tf_op jit(solution)/shard_map/ppermute | solution.py:78
  566.9 43.4 %reduce-scatter.27.cloned.1.call-done = bf16[128,1024]{1,0:T(8,128)(2,1)} async-done(((bf16[1024,1024]{1,0:T(8,128)(2,1)}), bf16[128,1024]{1,0:T(8,128)(2,1)}) %reduce-scatter.27.cloned.1.call-update) | async-done | bytes 262160
  611.5 7.3 all_gather.51
  620.1 40.8 %all-reduce.4 = (f32[1024]{0:T(1024)}, f32[1024]{0:T(1024)}, f32[4096]{0:T(1024)}, f32[4096]{0:T(1024)}, f32[1024]{0:T(1024)}) all-reduce(f32[1024]{0:T(1024)S(1)} %dynamic_update_slice.9, f32[1024]{0:T(1024)S(1)} %copy-done.44, f32[4096]{0:T(1024)S(1)} %dynamic_update_slice.10, ...), channel_id=1, replica_groups=mesh['fsdp'=4,'ctx'=2,'tp'=4] {'fsdp','ctx','tp'}, use_global_device_ids=true, to_apply=%region_23.24 | all-reduce | flops 11264 | bytes 90112 | tf_op jit(solution)/shard_map/psum | solution.py:248
  660.9 14.6 %reduce-scatter.25.cloned.1.call-done = bf16[128,256]{1,0:T(8,128)(2,1)} async-done(((bf16[1024,256]{1,0:T(8,128)(2,1)}), bf16[128,256]{1,0:T(8,128)(2,1)}) %reduce-scatter.25.cloned.1.call-update) | async-done | bytes 65552
  676.4 5.0 all_gather.49
  682.1 15.0 %all-gather.23.cloned.1.call-done = bf16[256,2048]{1,0:T(8,128)(2,1)} async-done(((bf16[128,2048]{1,0:T(8,128)(2,1)}), bf16[256,2048]{1,0:T(8,128)(2,1)}) %all-gather.23.cloned.1.call-update) | async-done | bytes 1048592 | tf_op jit(solution)/shard_map/all_gather | solution.py:223
  697.2 2.8 fusion.51
  699.9 30.8 %reduce-scatter.19.cloned.1.call-done = bf16[2,128,1024]{2,1,0:T(8,128)(2,1)} async-done(((bf16[2,512,1024]{2,1,0:T(8,128)(2,1)}), bf16[2,128,1024]{2,1,0:T(8,128)(2,1)}) %reduce-scatter.19.cloned.1.call-update) | async-done | bytes 524304 | tf_op jit(solution)/shard_map/reduce_scatter | solution.py:60
  732.0 1.5 collective-permute-start.3
  733.6 66.1 %reduce-scatter.21.cloned.1.call-done = bf16[128,768]{1,0:T(8,128)(2,1)} async-done(((bf16[1024,768]{1,0:T(8,128)(2,1)}), bf16[128,768]{1,0:T(8,128)(2,1)}) %reduce-scatter.21.cloned.1.call-update) | async-done | bytes 196624 | tf_op jit(solution)/shard_map/reduce_scatter | solution.py:220
  799.7 6.5 all_gather.48
  (217 shorter events, 32.5 us)
Async XLA Ops:
  7.2 14.3 %copy-start.55 = (f32[256]{0:T(256)S(1)}, f32[256]{0:T(256)}, u32[]{:S(2)}) copy-start(f32[256]{0:T(256)} %param.21) | copy-start | bytes 3076
  7.2 14.4 %copy-start.51 = (s32[2,512]{1,0:T(2,128)S(1)}, s32[2,512]{1,0:T(2,128)}, u32[]{:S(2)}) copy-start(s32[2,512]{1,0:T(2,128)} %param.30) | copy-start | bytes 12292
  7.2 18.7 %copy-start.54 = (s32[2,1024]{1,0:T(2,128)S(1)}, s32[2,1024]{1,0:T(2,128)}, u32[]{:S(2)}) copy-start(s32[2,1024]{1,0:T(2,128)} %param.29) | copy-start | bytes 24580
  7.2 18.7 %copy-start.32 = (bf16[256,256]{1,0:T(8,128)(2,1)S(1)}, bf16[256,256]{1,0:T(8,128)(2,1)}, u32[]{:S(2)}) copy-start(bf16[256,256]{1,0:T(8,128)(2,1)} %param.20) | copy-start | bytes 393220
  7.2 51.2 %all-gather.11.cloned.1.call-start = ((), (), s32[]{:S(2)}) async-start(), calls=%async_computation.9 | async-start | bytes 1966080 | tf_op jit(solution)/shard_map/all_gather | solution.py:152
  9.1 72.9 %all-gather.9.cloned.1.call-start = ((), (), s32[]{:S(2)}) async-start(), calls=%async_computation.8 | async-start | bytes 2621440 | tf_op jit(solution)/shard_map/all_gather | solution.py:56
  10.2 9.3 %collective-permute-start = (bf16[128,1024]{1,0:T(8,128)(2,1)S(1)}, bf16[128,1024]{1,0:T(8,128)(2,1)S(1)}, u32[]{:S(2)}, u32[]{:S(2)}) collective-permute-start(bf16[128,1024]{1,0:T(8,128)(2,1)S(1)} %dynamic-slice_bitcast_fusion.3), channel_id=1, source_target_pairs={{0,4},{4,0},{1,5},{5,1},{2,6},{6,2},{3,7},{7,3},{8,12},{12,8},{9,1... | collective-permute-start | bytes 786440 | tf_op jit(solution)/shard_map/ppermute | solution.py:78
  20.5 316.0 %copy-start.5 = (bf16[1,128,1024]{2,1,0:T(8,128)(2,1)}, bf16[1,128,1024]{2,1,0:T(8,128)(2,1)S(1)}, u32[]{:S(2)}) copy-start(bf16[1,128,1024]{2,1,0:T(8,128)(2,1)S(1)} %get-tuple-element.55) | copy-start | bytes 786436
  21.4 124.8 %reduce-scatter.13.cloned.1.call-start = ((), (), s32[]{:S(2)}) async-start(), calls=%async_computation.10 | async-start | bytes 2621440 | tf_op jit(solution)/shard_map/reduce_scatter | solution.py:60
  21.6 65.9 %copy-start.33 = (f32[4,64]{1,0:T(4,128)}, f32[4,64]{1,0:T(4,128)S(1)}, u32[]{:S(2)}) copy-start(f32[4,64]{1,0:T(4,128)S(1)} %mul.511) | copy-start | bytes 3076
  49.2 63.5 %copy-start.15 = (bf16[256,1024]{1,0:T(8,128)(2,1)}, bf16[256,1024]{1,0:T(8,128)(2,1)S(1)}, u32[]{:S(2)}) copy-start(bf16[256,1024]{1,0:T(8,128)(2,1)S(1)} %all_gather.42) | copy-start | bytes 1572868
  49.8 36.4 %copy-start.19 = (f32[1024,32]{0,1:T(8,128)}, f32[1024,32]{0,1:T(8,128)S(1)}, u32[]{:S(2)}) copy-start(f32[1024,32]{0,1:T(8,128)S(1)} %get-tuple-element.66) | copy-start | bytes 393220
  86.0 17.2 %copy-start.14 = (bf16[1024,256]{0,1:T(8,128)(2,1)}, bf16[1024,256]{0,1:T(8,128)(2,1)S(1)}, u32[]{:S(2)}) copy-start(bf16[1024,256]{0,1:T(8,128)(2,1)S(1)} %split.60) | copy-start | bytes 1572868
  86.5 8.6 %copy-start.2 = (f32[1024,4,32]{0,2,1:T(8,128)}, f32[1024,4,32]{0,2,1:T(8,128)S(1)}, u32[]{:S(2)}) copy-start(f32[1024,4,32]{0,2,1:T(8,128)S(1)} %get-tuple-element.64) | copy-start | bytes 1572868
  86.7 8.5 %copy-start.22 = (f32[1024,4]{0,1:T(4,128)}, f32[1024,4]{0,1:T(4,128)S(1)}, u32[]{:S(2)}) copy-start(f32[1024,4]{0,1:T(4,128)S(1)} %fusion.38) | copy-start | bytes 49156
  87.4 7.7 copy-start.28
  95.2 8.0 copy-start.35
  103.2 8.2 %copy-start.37 = (f32[4,1024]{1,0:T(4,128)}, f32[4,1024]{1,0:T(4,128)S(1)}, u32[]{:S(2)}) copy-start(f32[4,1024]{1,0:T(4,128)S(1)} %fusion) | copy-start | bytes 49156
  112.8 35.2 %copy-start.25 = (f32[1024]{0:T(1024)S(1)}, f32[1024]{0:T(1024)}, u32[]{:S(2)}) copy-start(f32[1024]{0:T(1024)} %param.22) | copy-start | bytes 12292
  114.9 114.1 %all-gather.15.cloned.1.call-start = ((), (), s32[]{:S(2)}) async-start(), calls=%async_computation.12 | async-start | bytes 5242880 | tf_op jit(solution)/shard_map/all_gather | solution.py:155
  117.2 134.8 %all-gather.13.cloned.1.call-start = ((), (), s32[]{:S(2)}) async-start(), calls=%async_computation.11 | async-start | bytes 2621440 | tf_op jit(solution)/shard_map/all_gather | solution.py:56
  148.0 111.0 %copy-start.39 = (f32[2,128]{1,0:T(2,128)}, f32[2,128]{1,0:T(2,128)S(1)}, u32[]{:S(2)}) copy-start(f32[2,128]{1,0:T(2,128)S(1)} %fusion.39) | copy-start | bytes 3076
  149.6 102.5 %copy-start.49 = (f32[2,128]{1,0:T(2,128)}, f32[2,128]{1,0:T(2,128)S(1)}, u32[]{:S(2)}) copy-start(f32[2,128]{1,0:T(2,128)S(1)} %multiply_reduce_fusion.7) | copy-start | bytes 3076
  149.6 109.5 %copy-start.41 = (f32[2,128]{1,0:T(2,128)}, f32[2,128]{1,0:T(2,128)S(1)}, u32[]{:S(2)}) copy-start(f32[2,128]{1,0:T(2,128)S(1)} %fusion.40) | copy-start | bytes 3076
  151.9 147.9 %all-gather.17.cloned.1.call-start = ((), (), s32[]{:S(2)}) async-start(), calls=%async_computation.13 | async-start | bytes 2621440 | tf_op jit(solution)/shard_map/all_gather | solution.py:156
  152.4 182.7 %reduce-scatter.15.cloned.1.call-start = ((), (), s32[]{:S(2)}) async-start(), calls=%async_computation.14 | async-start | bytes 2621440 | tf_op jit(solution)/shard_map/reduce_scatter | solution.py:60
  252.1 10.3 %copy-start.45 = (f32[1024]{0:T(1024)S(1)}, f32[1024]{0:T(1024)}, u32[]{:S(2)}) copy-start(f32[1024]{0:T(1024)} %param.27) | copy-start | bytes 12292
  252.1 10.3 %copy-start.50 = (f32[1024]{0:T(1024)S(1)}, f32[1024]{0:T(1024)}, u32[]{:S(2)}) copy-start(f32[1024]{0:T(1024)} %param.26) | copy-start | bytes 12292
  264.7 41.1 %copy-start.24 = (bf16[2,128,1024]{2,1,0:T(8,128)(2,1)S(1)}, bf16[2,128,1024]{2,1,0:T(8,128)(2,1)}, u32[]{:S(2)}) copy-start(bf16[2,128,1024]{2,1,0:T(8,128)(2,1)} %param.31) | copy-start | bytes 1572868
  305.7 30.8 %copy-start.1 = (bf16[2,128,1024]{2,1,0:T(8,128)(2,1)S(1)}, bf16[2,128,1024]{2,1,0:T(8,128)(2,1)}, u32[]{:S(2)}) copy-start(bf16[2,128,1024]{2,1,0:T(8,128)(2,1)} %reduce-scatter.13.cloned.1.call-done) | copy-start | bytes 1572868
  305.7 59.8 %all-gather.19.cloned.1.call-start = ((), (), s32[]{:S(2)}) async-start(), calls=%async_computation.15 | async-start | bytes 2621440 | tf_op jit(solution)/shard_map/all_gather | solution.py:56
  305.8 7.9 collective-permute-start.2
  314.7 23.8 %copy-start.10 = (bf16[1,128,1024]{2,1,0:T(8,128)(2,1)}, bf16[1,128,1024]{2,1,0:T(8,128)(2,1)S(1)}, u32[]{:S(2)}) copy-start(bf16[1,128,1024]{2,1,0:T(8,128)(2,1)S(1)} %get-tuple-element.56) | copy-start | bytes 786436
  314.7 23.8 %copy-start.11 = (bf16[1,128,1024]{2,1,0:T(8,128)(2,1)}, bf16[1,128,1024]{2,1,0:T(8,128)(2,1)S(1)}, u32[]{:S(2)}) copy-start(bf16[1,128,1024]{2,1,0:T(8,128)(2,1)S(1)} %get-tuple-element.57) | copy-start | bytes 786436
  342.7 73.0 %reduce-scatter.17.cloned.1.call-start = ((), (), s32[]{:S(2)}) async-start(), calls=%async_computation.16 | async-start | bytes 2621440 | tf_op jit(solution)/shard_map/reduce_scatter | solution.py:60
  365.5 9.4 %copy-start.46 = (f32[1024]{0:T(1024)S(1)}, f32[1024]{0:T(1024)}, u32[]{:S(2)}) copy-start(f32[1024]{0:T(1024)} %param.27) | copy-start | bytes 12292
  374.9 9.5 %copy-start.59 = (bf16[1024,1024]{1,0:T(8,128)(2,1)}, bf16[1024,1024]{1,0:T(8,128)(2,1)S(1)}, u32[]{:S(2)}) copy-start(bf16[1024,1024]{1,0:T(8,128)(2,1)S(1)} %get-tuple-element.36) | copy-start | bytes 6291460
  375.5 8.9 %copy-start.18 = (bf16[1024,1024]{1,0:T(8,128)(2,1)}, bf16[1024,1024]{1,0:T(8,128)(2,1)S(1)}, u32[]{:S(2)}) copy-start(bf16[1024,1024]{1,0:T(8,128)(2,1)S(1)} %multiply_convert_fusion.1) | copy-start | bytes 6291460
  384.4 62.3 %all-gather.21.cloned.1.call-start = ((), (), s32[]{:S(2)}) async-start(), calls=%async_computation.17 | async-start | bytes 2621440 | tf_op jit(solution)/shard_map/all_gather | solution.py:56
  415.7 7.2 copy-start.26
  415.7 7.2 copy-start.40
  424.0 114.7 %reduce-scatter.23.cloned.1.call-start = ((), (), s32[]{:S(2)}) async-start(), calls=%async_computation.20 | async-start | bytes 4718592 | tf_op jit(solution)/shard_map/reduce_scatter | solution.py:220
  433.5 176.9 %reduce-scatter.27.cloned.1.call-start = ((), (), s32[]{:S(2)}) async-start(), calls=%async_computation.23 | async-start | bytes 2359296
  440.1 6.6 copy-start.16
  444.1 231.3 %reduce-scatter.25.cloned.1.call-start = ((), (), s32[]{:S(2)}) async-start(), calls=%async_computation.22 | async-start | bytes 589824
  449.2 16.7 %copy-start.12 = (bf16[1024,256]{0,1:T(8,128)(2,1)}, bf16[1024,256]{0,1:T(8,128)(2,1)S(1)}, u32[]{:S(2)}) copy-start(bf16[1024,256]{0,1:T(8,128)(2,1)S(1)} %convolution_convert_fusion.7) | copy-start | bytes 1572868
  452.2 13.7 %slice-start = ((s8[16777216]{0:T(1024)(128)(4,1)}), s8[4194304]{0:T(1024)(128)(4,1)S(1)}, s32[]{:S(2)}) async-start(s8[16777216]{0:T(1024)(128)(4,1)} %bitcast.128), calls=%async_computation.24 | async-start | bytes 8388608
  452.2 14.8 %slice-start.1 = ((s8[16777216]{0:T(1024)(128)(4,1)}), s8[4194304]{0:T(1024)(128)(4,1)S(1)}, s32[]{:S(2)}) async-start(s8[16777216]{0:T(1024)(128)(4,1)} %bitcast.128), calls=%async_computation.25 | async-start | bytes 8388608
  452.2 16.0 %slice-start.2 = ((s8[16777216]{0:T(1024)(128)(4,1)}), s8[4194304]{0:T(1024)(128)(4,1)S(1)}, s32[]{:S(2)}) async-start(s8[16777216]{0:T(1024)(128)(4,1)} %bitcast.128), calls=%async_computation.26 | async-start | bytes 8388608
  452.2 17.3 %slice-start.3 = ((s8[16777216]{0:T(1024)(128)(4,1)}), s8[4194304]{0:T(1024)(128)(4,1)S(1)}, s32[]{:S(2)}) async-start(s8[16777216]{0:T(1024)(128)(4,1)} %bitcast.128), calls=%async_computation.27 | async-start | bytes 8388608
  469.4 10.9 %copy-start.3 = (f32[1024,4,32]{0,2,1:T(8,128)S(1)}, f32[1024,4,32]{0,2,1:T(8,128)}, u32[]{:S(2)}) copy-start(f32[1024,4,32]{0,2,1:T(8,128)} %copy-done.2) | copy-start | bytes 1572868
  489.8 207.4 %all-gather.23.cloned.1.call-start = ((), (), s32[]{:S(2)}) async-start(), calls=%async_computation.21 | async-start | bytes 1572864 | tf_op jit(solution)/shard_map/all_gather | solution.py:223
  492.0 47.0 %copy-start.13 = (bf16[1024,256]{0,1:T(8,128)(2,1)S(1)}, bf16[1024,256]{0,1:T(8,128)(2,1)}, u32[]{:S(2)}) copy-start(bf16[1024,256]{0,1:T(8,128)(2,1)} %copy-done.12) | copy-start | bytes 1572868
  538.7 192.1 %reduce-scatter.19.cloned.1.call-start = ((), (), s32[]{:S(2)}) async-start(), calls=%async_computation.18 | async-start | bytes 2621440 | tf_op jit(solution)/shard_map/reduce_scatter | solution.py:60
  539.0 8.6 %copy-start.58 = (bf16[1024,768]{1,0:T(8,128)(2,1)S(1)}, bf16[1024,768]{1,0:T(8,128)(2,1)}, u32[]{:S(2)}) copy-start(bf16[1024,768]{1,0:T(8,128)(2,1)} %all-gather.11.cloned.1.call-done) | copy-start | bytes 4718596
  550.8 248.9 %reduce-scatter.21.cloned.1.call-start = ((), (), s32[]{:S(2)}) async-start(), calls=%async_computation.19 | async-start | bytes 1769472 | tf_op jit(solution)/shard_map/reduce_scatter | solution.py:220
  555.5 10.8 %copy-start.53 = (f32[1024]{0:T(1024)S(1)}, f32[1024]{0:T(1024)}, u32[]{:S(2)}) copy-start(f32[1024]{0:T(1024)} %get-tuple-element.14) | copy-start | bytes 12292
  555.5 11.1 %copy-start.52 = (f32[1024]{0:T(1024)S(1)}, f32[1024]{0:T(1024)}, u32[]{:S(2)}) copy-start(f32[1024]{0:T(1024)} %get-tuple-element.15) | copy-start | bytes 12292
  555.5 64.6 %copy-start.43 = (f32[1024]{0:T(1024)S(1)}, f32[1024]{0:T(1024)}, u32[]{:S(2)}) copy-start(f32[1024]{0:T(1024)} %get-tuple-element.16) | copy-start | bytes 12292
  555.5 64.6 %copy-start.44 = (f32[1024]{0:T(1024)S(1)}, f32[1024]{0:T(1024)}, u32[]{:S(2)}) copy-start(f32[1024]{0:T(1024)} %get-tuple-element.22) | copy-start | bytes 12292
  555.6 9.8 %collective-permute-start.1 = (bf16[128,1024]{1,0:T(8,128)(2,1)S(1)}, bf16[128,1024]{1,0:T(8,128)(2,1)S(1)}, u32[]{:S(2)}, u32[]{:S(2)}) collective-permute-start(bf16[128,1024]{1,0:T(8,128)(2,1)S(1)} %dynamic-slice_bitcast_fusion.2), channel_id=1, source_target_pairs={{0,4},{4,0},{1,5},{5,1},{2,6},{6,2},{3,7},{7,3},{8,12},{12,8},{9,1... | collective-permute-start | bytes 786440 | tf_op jit(solution)/shard_map/ppermute | solution.py:78
  566.3 164.5 %copy-start.7 = (f32[2,128,1024]{2,1,0:T(8,128)S(1)}, f32[2,128,1024]{2,1,0:T(8,128)}, u32[]{:S(2)}) copy-start(f32[2,128,1024]{2,1,0:T(8,128)} %copy-done.6) | copy-start | bytes 3145732
  566.3 164.5 %copy-start.27 = (f32[1024]{0:T(1024)S(1)}, f32[1024]{0:T(1024)}, u32[]{:S(2)}) copy-start(f32[1024]{0:T(1024)} %param.22) | copy-start | bytes 12292
  732.0 75.1 %collective-permute-start.3 = (bf16[128,1024]{1,0:T(8,128)(2,1)S(1)}, bf16[128,1024]{1,0:T(8,128)(2,1)S(1)}, u32[]{:S(2)}, u32[]{:S(2)}) collective-permute-start(bf16[128,1024]{1,0:T(8,128)(2,1)S(1)} %dynamic-slice_bitcast_fusion), channel_id=1, source_target_pairs={{0,4},{4,0},{1,5},{5,1},{2,6},{6,2},{3,7},{7,3},{8,12},{12,8},{9,1... | collective-permute-start | bytes 786440 | tf_op jit(solution)/shard_map/ppermute | solution.py:78
  (20 other events, 60.6 us)
Sparse Core Ops, SparseCore 0:
  10.2 48.1 all-gather.10
  60.5 21.4 all-gather.8
  115.0 31.1 reduce-scatter.12
  148.2 80.7 all-gather.14
  231.0 21.0 all-gather.12
  253.5 46.2 all-gather.16
  305.8 29.3 reduce-scatter.14
  342.9 22.5 all-gather.18
  384.5 31.1 reduce-scatter.16
  424.1 22.5 all-gather.20
  450.3 88.2 reduce-scatter.22
  542.1 68.2 reduce-scatter.26
  613.7 61.7 reduce-scatter.24
  676.9 20.2 all-gather.22
  699.5 31.1 reduce-scatter.18
  734.0 65.5 reduce-scatter.20
